TPU v7x, 256 devices: a whole 4x4x8 slice. The times are simulated.
256 devices in a mesh: dp: 32 (over x, y, z_hi), mp: 8 (over z_lo, core).
Axes of the slice: x: 4, y: 4, z: 8 (z_hi: 2, z_lo: 4; z = z_hi * 4 + z_lo), core: 2. Of those that a mesh axis runs over, the one named last changes fastest.
Arguments:
- tokens: bfloat16 [1024, 7168], P('dp', 'mp'), may hold values from -6 to 6
- gate_weight: bfloat16 [7168, 18432], P('mp', 'dp'), may hold values from -0.0625 to 0.0625
- up_weight: bfloat16 [7168, 18432], P('mp', 'dp'), may hold values from -0.0625 to 0.0625
- down_weight: bfloat16 [18432, 7168], P('dp', 'mp'), may hold values from -0.046875 to 0.046875
- gate_round: bfloat16 [7168, 18432], P('mp', 'dp'), may hold values from -8 to 8
- up_round: bfloat16 [7168, 18432], P('mp', 'dp'), may hold values from -8 to 8
- down_round: bfloat16 [18432, 7168], P('dp', 'mp'), may hold values from -8 to 8
- quant_scale: float32 [2, 18432], P(None, 'dp'), may hold values from 0.3 to 3
- quant_bits: int32 [2, 18432], P(None, 'dp'), may hold values from 2 to 4
- quant_zero: int32 [2, 18432], P(None, 'dp'), may hold values from 0 to 2
- down_scale: float32 [7168], P('mp'), may hold values from 0.3 to 3
- down_bits: int32 [7168], P('mp'), may hold values from 2 to 4
- down_zero: int32 [7168], P('mp'), may hold values from 0 to 2
- fisher: float32 [1024], replicated, may hold values from 1 to 300, as said below
Outputs:
- loss_value: float32 [], replicated
- grad_gate: bfloat16 [7168, 18432], P('mp', 'dp')
- grad_up: bfloat16 [7168, 18432], P('mp', 'dp')
- grad_down: bfloat16 [18432, 7168], P('dp', 'mp')
Inputs may be any that keep to these rules, and one draw needn't show every extreme that they name: `fisher`: positive weights.
All inputs are finite; a program needn't handle non-finite values.
Results may differ from a plain program's by a relative error of at most 0.0059.
Values may be sent and summed in bfloat16 or wider, within the bound.
No kernel may reach another device: no remote copies, remote signals or barrier semaphores. Data moves between devices by JAX's collectives and lax.ppermute only.
A program may use at most 128 MiB of HBM per device.

v0:
```python
import jax
import jax.numpy as jnp
from jax import lax
from jax.sharding import Mesh
from jax.sharding import PartitionSpec as P

D = 7168
FF = 18432
DP = ("dp_0", "dp_1", "dp_2")
MP = ("mp_0", "mp_1")
DP_MP = ("dp_0", "dp_1", "dp_2", "mp_0", "mp_1")


def in_order(tiles, dim):
    tiles = jnp.moveaxis(tiles, 0, dim)
    shape = tiles.shape
    return tiles.reshape(*shape[:dim], shape[dim] * shape[dim + 1], *shape[dim + 2 :])


def copy_for_each(value, axis):
    copies = jnp.broadcast_to(value, (lax.axis_size(axis), *value.shape))
    return lax.all_to_all(copies, axis, split_axis=0, concat_axis=0, tiled=True)


def gathered_copies(value, axis, dim):
    return in_order(copy_for_each(value, axis), dim)


def scatter_axes(value, axes, dim):
    if not axes:
        return value
    nearer = lax.psum_scatter(value, axes[0], scatter_dimension=dim, tiled=True)
    return scatter_axes(nearer, axes[1:], dim)


def over_axes(value, axes):
    for axis in axes:
        value = lax.psum(value, axis)
    return value


def split_up(value, dim, count):
    shape = value.shape
    tiles = value.reshape(*shape[:dim], count, shape[dim] // count, *shape[dim + 1 :])
    return jnp.moveaxis(tiles, dim, 0)


def sent_and_summed(value, axis, dim):
    count = lax.axis_size(axis)
    tiles = lax.all_to_all(split_up(value, dim, count), axis, 0, 0, tiled=True)
    return jnp.sum(tiles, axis=0)


def soft_weight(weight, variable, channel_scale, bit_width, zero_point, fan_in):
    quant_step = channel_scale / jnp.sqrt(jnp.float32(fan_in))
    offset = jnp.clip(1.2 * jax.nn.sigmoid(variable.astype(jnp.float32)) - 0.1, 0.0, 1.0)
    ceiling = (jnp.left_shift(jnp.int32(1), bit_width) - 1).astype(jnp.float32)
    zero_level = zero_point.astype(jnp.float32)
    levels = jnp.clip(
        weight.astype(jnp.float32) / quant_step + offset - 0.5 + zero_level, 0.0, ceiling
    )
    return (quant_step * (levels - zero_level)).astype(jnp.bfloat16)


def contract_rows(left, right):
    return lax.dot_general(
        left, right, (((0,), (0,)), ((), ())), preferred_element_type=jnp.float32
    )


def shards(
    tokens,
    gate_weight,
    up_weight,
    down_weight,
    gate_round,
    up_round,
    down_round,
    quant_scale,
    quant_bits,
    quant_zero,
    down_scale,
    down_bits,
    down_zero,
    fisher,
):
    own_rows = tokens.shape[0]
    hidden_cols = gate_weight.shape[1]
    all_tokens = lax.all_gather(tokens, DP, axis=0, tiled=True)
    total_rows = all_tokens.shape[0]
    gate_student = soft_weight(
        gate_weight, gate_round, quant_scale[0], quant_bits[0], quant_zero[0], D
    )
    up_student = soft_weight(up_weight, up_round, quant_scale[1], quant_bits[1], quant_zero[1], D)
    stacked = jnp.concatenate([gate_weight, up_weight, gate_student, up_student], axis=1)
    partial_value = jnp.dot(all_tokens, stacked, preferred_element_type=jnp.float32)
    shares = lax.psum_scatter(partial_value, MP, scatter_dimension=0, tiled=True)
    gate_teacher = shares[:, :hidden_cols]
    up_teacher = shares[:, hidden_cols : 2 * hidden_cols]
    gate_own = shares[:, 2 * hidden_cols : 3 * hidden_cols]
    up_own = shares[:, 3 * hidden_cols :]
    hidden_teacher = (jax.nn.silu(gate_teacher) * up_teacher).astype(jnp.bfloat16)
    hidden_student = (jax.nn.silu(gate_own) * up_own).astype(jnp.bfloat16)
    hidden = gathered_copies(jnp.concatenate([hidden_teacher, hidden_student], axis=1), MP, 0)
    down_student = soft_weight(down_weight, down_round, down_scale, down_bits, down_zero, FF)
    terms = jnp.dot(
        hidden,
        jnp.concatenate([-down_weight, down_student], axis=0),
        preferred_element_type=jnp.float32,
    )
    summed = scatter_axes(terms, DP, 0)
    token_weight = lax.dynamic_slice_in_dim(fisher, lax.axis_index(DP) * own_rows, own_rows)
    weighted = token_weight[:, None] * summed
    partial_loss = jnp.sum(weighted * summed)
    local_grad = (2.0 * weighted).astype(jnp.bfloat16)
    loss_sum = over_axes(partial_loss, DP_MP)
    out_grad = lax.all_gather(local_grad, DP, axis=0, tiled=True)
    loss_value = loss_sum / (total_rows * D)
    grad_down = contract_rows(hidden[:, hidden_cols:], out_grad).astype(jnp.bfloat16)
    hidden_part = lax.dot_general(
        out_grad, down_student, (((1,), (1,)), ((), ())), preferred_element_type=jnp.float32
    )
    hidden_grad = sent_and_summed(hidden_part, MP, 0)
    sigmoid_gate = jax.nn.sigmoid(gate_own)
    gate_grad = (
        hidden_grad * up_own * sigmoid_gate * (1.0 + gate_own * (1.0 - sigmoid_gate))
    ).astype(jnp.bfloat16)
    up_grad = (hidden_grad * gate_own * sigmoid_gate).astype(jnp.bfloat16)
    both_grads = gathered_copies(jnp.concatenate([gate_grad, up_grad], axis=1), MP, 0)
    weight_grads = contract_rows(all_tokens, both_grads)
    grad_gate = weight_grads[:, :hidden_cols].astype(jnp.bfloat16)
    grad_up = weight_grads[:, hidden_cols:].astype(jnp.bfloat16)
    return (loss_value, grad_gate, grad_up, grad_down)


def solution(mesh):
    split = Mesh(mesh.devices.reshape(4, 4, 2, 4, 2), ("dp_0", "dp_1", "dp_2", "mp_0", "mp_1"))
    return jax.shard_map(
        shards,
        mesh=split,
        in_specs=(
            P(DP, MP),
            P(MP, DP),
            P(MP, DP),
            P(DP, MP),
            P(MP, DP),
            P(MP, DP),
            P(DP, MP),
            P(None, DP),
            P(None, DP),
            P(None, DP),
            P(MP),
            P(MP),
            P(MP),
            P(),
        ),
        out_specs=(P(), P(MP, DP), P(MP, DP), P(DP, MP)),
        check_vma=False,
    )
```

profile of v0, /device:TPU:65, one launch (start us, length us, event | category | flops | bytes accessed | tf_op | source)
XLA Modules:
  0.0 616.8 jit_solution(13538513241438266588)
XLA Ops:
  7.2 0.0 all-gather.3.cloned.1.call-start
  7.2 0.7 all-gather.3.cloned.1.call-update
  7.9 0.0 reduce-scatter.5.cloned.1.call-start
  7.9 0.8 convert_reduce_fusion.2
  8.7 0.8 multiply_reduce_fusion.1
  9.5 0.8 convert_reduce_fusion.3
  10.3 4.8 multiply_convert_fusion.1
  15.1 83.8 %all-gather.3.cloned.1.call-done = bf16[1024,896]{1,0:T(8,128)(2,1)} async-done(((bf16[32,896]{1,0:T(8,128)(2,1)}), bf16[1024,896]{1,0:T(8,128)(2,1)}) %all-gather.3.cloned.1.call-update) | async-done | bytes 1835024 | tf_op jit(solution)/shard_map/all_gather | solution.py:89
  99.0 11.9 %convolution_bitcast_fusion = f32[1024,2304]{0,1:T(8,128)} fusion(bf16[1024,896]{1,0:T(8,128)(2,1)} %all-gather.3.cloned.1.call-done, bf16[896,576]{0,1:T(8,128)(2,1)S(1)} %get-tuple-element.18, bf16[896,576]{0,1:T(8,128)(2,1)} %get-tuple-element.19, bf16[896,576]{0,1:T(8,128)(2,1)S(1)} %copy-done.6, bf16[896,576]{0,1:T(8,128)(2,1)S(1)} %copy-done.7), kind=kOutput, calls=%fused_computation | convolution fusion | flops 4244373504 | bytes 15400960 | tf_op jit(solution)/shard_map/dot_general | solution.py:96
  110.9 0.0 reduce-scatter.5.cloned.1.call-update
  110.9 100.8 %reduce-scatter.5.cloned.1.call-done = f32[128,2304]{0,1:T(8,128)} async-done(((f32[1024,2304]{0,1:T(8,128)}), f32[128,2304]{0,1:T(8,128)}) %reduce-scatter.5.cloned.1.call-update) | async-done | bytes 1179664 | tf_op jit(solution)/shard_map/reduce_scatter | solution.py:97
  211.7 1.4 fusion.13
  213.1 0.2 copy.20
  213.3 1.7 broadcast_in_dim.8
  215.1 6.0 all-to-all-start
  221.0 0.0 reduce-scatter.7.cloned.1.call-start
  221.1 1.1 neg.24
  222.3 0.2 copy-done.4
  222.5 2.1 multiply_convert_fusion
  224.7 47.2 %all-to-all-done = bf16[8,128,1152]{2,1,0:T(8,128)(2,1)S(1)} async-done(((bf16[8,128,1152]{2,1,0:T(8,128)(2,1)}), bf16[8,128,1152]{2,1,0:T(8,128)(2,1)S(1)}, u32[]{:S(2)}, u32[]{:S(2)}) %all-to-all-start) | async-done | bytes 2359328 | tf_op jit(solution)/shard_map/all_to_all | solution.py:22
  271.9 7.0 %fusion.8 = f32[1024,896]{1,0:T(8,128)} fusion(bf16[1024,1152]{1,0:T(8,128)(2,1)S(1)} %bitcast.19, bf16[576,896]{1,0:T(8,128)(2,1)} %multiply_convert_fusion, bf16[576,896]{1,0:T(8,128)(2,1)} %neg.24), kind=kOutput, calls=%fused_computation.11 | convolution fusion | flops 2118057984 | bytes 8093696 | tf_op jit(solution)/shard_map/dot_general | solution.py:106
  278.9 0.0 reduce-scatter.7.cloned.1.call-update
  278.9 0.0 reduce-scatter.9.cloned.1.call-start
  279.0 47.4 %reduce-scatter.7.cloned.1.call-done = f32[256,896]{1,0:T(8,128)} async-done(((f32[1024,896]{1,0:T(8,128)}), f32[256,896]{1,0:T(8,128)}) %reduce-scatter.7.cloned.1.call-update) | async-done | bytes 917520 | tf_op jit(solution)/shard_map/reduce_scatter | solution.py:32
  326.4 0.0 reduce-scatter.11.cloned.1.call-start
  326.4 26.6 %reduce-scatter.9.cloned.1.call-done = f32[64,896]{1,0:T(8,128)} async-done(((f32[256,896]{1,0:T(8,128)}), f32[64,896]{1,0:T(8,128)}) %reduce-scatter.9.cloned.1.call-update) | async-done | bytes 229392 | tf_op jit(solution)/shard_map/reduce_scatter | solution.py:32
  353.1 0.0 all-gather.5.cloned.1.call-start
  353.1 0.8 dynamic_slice.3
  353.9 23.4 %reduce-scatter.11.cloned.1.call-done = f32[32,896]{1,0:T(8,128)} async-done(((f32[64,896]{1,0:T(8,128)}), f32[32,896]{1,0:T(8,128)}) %reduce-scatter.11.cloned.1.call-update) | async-done | bytes 114704 | tf_op jit(solution)/shard_map/reduce_scatter | solution.py:32
  377.2 2.2 fusion.15
  379.5 85.6 %all-gather.5.cloned.1.call-done = bf16[1024,896]{1,0:T(8,128)(2,1)} async-done(((bf16[32,896]{1,0:T(8,128)(2,1)}), bf16[1024,896]{1,0:T(8,128)(2,1)}) %all-gather.5.cloned.1.call-update) | async-done | bytes 1835024 | tf_op jit(solution)/shard_map/all_gather | solution.py:117
  465.0 2.9 convolution_bitcast_fusion.1
  468.0 0.2 copy.25
  468.1 57.4 %all_to_all.15 = f32[8,128,576]{1,2,0:T(8,128)S(1)} all-to-all(f32[8,128,576]{1,2,0:T(8,128)S(1)} %bitcast.18), channel_id=1, replica_groups=mesh['dp_0'=4,'dp_1'=4,'dp_2'=2,'mp_0'=4,'mp_1'=2] {'mp_0','mp_1'}, dimensions={0} | all-to-all | bytes 4718592 | tf_op jit(solution)/shard_map/all_to_all | solution.py:50
  525.6 0.8 reduce_sum.19
  526.4 0.5 copy-done.1
  526.9 1.1 multiply_convert_fusion.4
  528.1 0.2 copy.22
  528.3 1.7 broadcast_in_dim.9
  530.0 8.4 %all-to-all-start.2 = ((bf16[8,128,1152]{2,1,0:T(8,128)(2,1)}), bf16[8,128,1152]{2,1,0:T(8,128)(2,1)}, u32[]{:S(2)}, u32[]{:S(2)}) async-start(bf16[8,128,1152]{2,1,0:T(8,128)(2,1)} %broadcast_in_dim.9), calls=%async_computation.6 | async-start | bytes 4718592 | tf_op jit(solution)/shard_map/all_to_all | solution.py:22
  538.4 7.8 %psum.35 = f32[]{:T(128)} all-reduce(f32[]{:T(128)} %get-tuple-element.17), channel_id=1, replica_groups=mesh['dp_0'=4,'dp_1'=4,'dp_2'=2,'mp_0'=4,'mp_1'=2] {'dp_0'}, use_global_device_ids=true, to_apply=%region_5.6 | all-reduce | flops 1 | bytes 8 | tf_op jit(solution)/shard_map/psum | solution.py:38
  546.2 8.5 %psum.36 = f32[]{:T(128)} all-reduce(f32[]{:T(128)} %psum.35), channel_id=1, replica_groups=mesh['dp_0'=4,'dp_1'=4,'dp_2'=2,'mp_0'=4,'mp_1'=2] {'dp_1'}, use_global_device_ids=true, to_apply=%region_6.7 | all-reduce | flops 1 | bytes 8 | tf_op jit(solution)/shard_map/psum | solution.py:38
  554.7 14.7 %psum.37 = f32[]{:T(128)} all-reduce(f32[]{:T(128)} %psum.36), channel_id=1, replica_groups=mesh['dp_0'=4,'dp_1'=4,'dp_2'=2,'mp_0'=4,'mp_1'=2] {'dp_2'}, use_global_device_ids=true, to_apply=%region_7.8 | all-reduce | flops 1 | bytes 8 | tf_op jit(solution)/shard_map/psum | solution.py:38
  569.4 23.5 %psum.38 = f32[]{:T(128)} all-reduce(f32[]{:T(128)} %psum.37), channel_id=1, replica_groups=mesh['dp_0'=4,'dp_1'=4,'dp_2'=2,'mp_0'=4,'mp_1'=2] {'mp_0'}, use_global_device_ids=true, to_apply=%region_8.9 | all-reduce | flops 1 | bytes 8 | tf_op jit(solution)/shard_map/psum | solution.py:38
  592.9 4.9 psum.39
  598.5 4.0 convolution_convert_fusion.1
  602.5 4.9 fusion.7
  607.4 1.5 fusion.18
  (29 shorter events, 0.2 us)
Async XLA Ops:
  7.2 91.8 %all-gather.3.cloned.1.call-start = ((), (), s32[]{:S(2)}) async-start(), calls=%async_computation.7 | async-start | bytes 1892352 | tf_op jit(solution)/shard_map/all_gather | solution.py:89
  7.9 203.8 %reduce-scatter.5.cloned.1.call-start = ((), (), s32[]{:S(2)}) async-start(), calls=%async_computation.8 | async-start | bytes 10616832 | tf_op jit(solution)/shard_map/reduce_scatter | solution.py:97
  10.3 88.7 %copy-start.6 = (bf16[896,576]{0,1:T(8,128)(2,1)S(1)}, bf16[896,576]{0,1:T(8,128)(2,1)}, u32[]{:S(2)}) copy-start(bf16[896,576]{0,1:T(8,128)(2,1)} %param.16) | copy-start | bytes 3096580
  10.3 88.6 %copy-start.7 = (bf16[896,576]{0,1:T(8,128)(2,1)S(1)}, bf16[896,576]{0,1:T(8,128)(2,1)}, u32[]{:S(2)}) copy-start(bf16[896,576]{0,1:T(8,128)(2,1)} %param.15) | copy-start | bytes 3096580
  215.1 6.0 copy-start.8
  215.1 6.1 copy-start
  215.1 56.8 %all-to-all-start = ((bf16[8,128,1152]{2,1,0:T(8,128)(2,1)}), bf16[8,128,1152]{2,1,0:T(8,128)(2,1)S(1)}, u32[]{:S(2)}, u32[]{:S(2)}) async-start(bf16[8,128,1152]{2,1,0:T(8,128)(2,1)} %broadcast_in_dim.8), calls=%async_computation.1 | async-start | bytes 4718592 | tf_op jit(solution)/shard_map/all_to_all | solution.py:22
  221.0 1.2 copy-start.9
  221.0 1.2 copy-start.10
  221.0 105.3 %reduce-scatter.7.cloned.1.call-start = ((), (), s32[]{:S(2)}) async-start(), calls=%async_computation.9 | async-start | bytes 4587520 | tf_op jit(solution)/shard_map/reduce_scatter | solution.py:32
  221.1 1.4 copy-start.4
  271.9 7.0 %copy-start.2 = (bf16[8,128,1152]{2,1,0:T(8,128)(2,1)}, bf16[8,128,1152]{2,1,0:T(8,128)(2,1)S(1)}, u32[]{:S(2)}) copy-start(bf16[8,128,1152]{2,1,0:T(8,128)(2,1)S(1)} %all-to-all-done) | copy-start | bytes 7077892
  278.9 186.2 %copy-start.5 = (bf16[576,896]{1,0:T(8,128)(2,1)S(1)}, bf16[576,896]{1,0:T(8,128)(2,1)}, u32[]{:S(2)}) copy-start(bf16[576,896]{1,0:T(8,128)(2,1)} %multiply_convert_fusion) | copy-start | bytes 3096580
  278.9 74.1 %reduce-scatter.9.cloned.1.call-start = ((), (), s32[]{:S(2)}) async-start(), calls=%async_computation.10 | async-start | bytes 1146880 | tf_op jit(solution)/shard_map/reduce_scatter | solution.py:32
  326.4 50.8 %reduce-scatter.11.cloned.1.call-start = ((), (), s32[]{:S(2)}) async-start(), calls=%async_computation.11 | async-start | bytes 344064 | tf_op jit(solution)/shard_map/reduce_scatter | solution.py:32
  353.1 112.0 %all-gather.5.cloned.1.call-start = ((), (), s32[]{:S(2)}) async-start(), calls=%async_computation.12 | async-start | bytes 1892352 | tf_op jit(solution)/shard_map/all_gather | solution.py:117
  525.6 1.4 copy-start.1
  530.0 68.5 %copy-start.3 = (bf16[8,128,1152]{2,1,0:T(8,128)(2,1)S(1)}, bf16[8,128,1152]{2,1,0:T(8,128)(2,1)}, u32[]{:S(2)}) copy-start(bf16[8,128,1152]{2,1,0:T(8,128)(2,1)} %copy-done.2) | copy-start | bytes 7077892
  530.0 72.5 %all-to-all-start.2 = ((bf16[8,128,1152]{2,1,0:T(8,128)(2,1)}), bf16[8,128,1152]{2,1,0:T(8,128)(2,1)}, u32[]{:S(2)}, u32[]{:S(2)}) async-start(bf16[8,128,1152]{2,1,0:T(8,128)(2,1)} %broadcast_in_dim.9), calls=%async_computation.6 | async-start | bytes 4718592 | tf_op jit(solution)/shard_map/all_to_all | solution.py:22
Sparse Core Ops, SparseCore 0:
  11.4 87.5 all-gather.2
  111.0 100.6 reduce-scatter.4
  279.0 47.2 reduce-scatter.6
  328.8 24.2 reduce-scatter.8
  355.4 21.8 reduce-scatter.10
  381.1 83.9 all-gather.4
where the time goes:
time: 618 us; the launch traced here: 617 us
  waiting for transfers between devices  415 us (67%)
  blocking collectives  117 us (19%)
  matrix products  30.7 us (5%)
  other arithmetic  16 us (3%)
  between operations  16 us (3%)
  starting transfers between devices  14.6 us (2%)
  local copies, waits for them, and re-layouts  7.04 us (1%)
    reduce_scatter x1, waiting for transfers between devices, shards(): lax.psum_scatter(partial_value, MP, scatter_dimension=0, tiled=True)  101 us
    reduce_scatter x3, waiting for transfers between devices, scatter_axes(): nearer = lax.psum_scatter(value, axes[0], scatter_dimension=dim, tiled=True)  97.4 us
    all_gather x1, waiting for transfers between devices, shards(): out_grad = lax.all_gather(local_grad, DP, axis=0, tiled=True)  85.6 us
    all_gather x1, waiting for transfers between devices, shards(): all_tokens = lax.all_gather(tokens, DP, axis=0, tiled=True)  83.8 us
    psum x5, blocking collectives, over_axes(): value = lax.psum(value, axis)  59.4 us
    all_to_all x1, blocking collectives, sent_and_summed(): tiles = lax.all_to_all(split_up(value, dim, count), axis, 0, 0, tiled=True)  57.4 us
    all_to_all x2, waiting for transfers between devices, copy_for_each(): return lax.all_to_all(copies, axis, split_axis=0, concat_axis=0, tiled=True)  47.2 us
    all_to_all x2, starting transfers between devices, copy_for_each(): return lax.all_to_all(copies, axis, split_axis=0, concat_axis=0, tiled=True)  14.4 us
  transfers between devices with their start and end apart: 8, of which 7 were waited for; matrix products, arithmetic and copies ran while one was open for 2% of the time, Pallas kernels for 0%

commit v1 on v0

--- a/solution.py
+++ b/solution.py
@@ -86,7 +86,9 @@
 ):
     own_rows = tokens.shape[0]
     hidden_cols = gate_weight.shape[1]
-    all_tokens = lax.all_gather(tokens, DP, axis=0, tiled=True)
+    all_tokens = jnp.concatenate(
+        lax.all_to_all(jnp.stack([tokens] * lax.axis_size(DP)), DP, 0, 0), axis=0
+    )
     total_rows = all_tokens.shape[0]
     gate_student = soft_weight(
         gate_weight, gate_round, quant_scale[0], quant_bits[0], quant_zero[0], D

time: 618 us -> 587 us (0.950)
  waiting for transfers between devices: 415 us -> 373 us
  starting transfers between devices: 14.6 us -> 26.7 us
    all_gather x1 -> x0, waiting for transfers between devices: 83.8 us -> none  [shards(): all_tokens = lax.all_gather(tokens, DP, axis=0, tiled=True)]
    all_to_all x0 -> x1, waiting for transfers between devices: none -> 44.1 us  [shards(): lax.all_to_all(jnp.stack([tokens] * lax.axis_size(DP)), DP, 0, 0)]
    all_to_all x0 -> x1, starting transfers between devices: none -> 12 us  [shards(): lax.all_to_all(jnp.stack([tokens] * lax.axis_size(DP)), DP, 0, 0)]
where the time goes in v1:
time: 587 us; the launch traced here: 586 us
  waiting for transfers between devices  373 us (64%)
  blocking collectives  117 us (20%)
  matrix products  30.4 us (5%)
  starting transfers between devices  26.7 us (5%)
  between operations  15.7 us (3%)
  other arithmetic  13.8 us (2%)
  local copies, waits for them, and re-layouts  9.25 us (2%)
    reduce_scatter x1, waiting for transfers between devices, shards(): lax.psum_scatter(partial_value, MP, scatter_dimension=0, tiled=True)  98.8 us
    reduce_scatter x3, waiting for transfers between devices, scatter_axes(): nearer = lax.psum_scatter(value, axes[0], scatter_dimension=dim, tiled=True)  97.3 us
    all_gather x1, waiting for transfers between devices, shards(): out_grad = lax.all_gather(local_grad, DP, axis=0, tiled=True)  85.6 us
    psum x5, blocking collectives, over_axes(): value = lax.psum(value, axis)  59.4 us
    all_to_all x1, blocking collectives, sent_and_summed(): tiles = lax.all_to_all(split_up(value, dim, count), axis, 0, 0, tiled=True)  57.4 us
    all_to_all x2, waiting for transfers between devices, copy_for_each(): return lax.all_to_all(copies, axis, split_axis=0, concat_axis=0, tiled=True)  47.2 us
    all_to_all x1, waiting for transfers between devices, shards(): lax.all_to_all(jnp.stack([tokens] * lax.axis_size(DP)), DP, 0, 0)  44.1 us
    all_to_all x2, starting transfers between devices, copy_for_each(): return lax.all_to_all(copies, axis, split_axis=0, concat_axis=0, tiled=True)  14.4 us
  transfers between devices with their start and end apart: 8, of which 7 were waited for; matrix products, arithmetic and copies ran while one was open for 2% of the time, Pallas kernels for 0%

profile of v1, /device:TPU:65, one launch (start us, length us, event | category | flops | bytes accessed | tf_op | source)
XLA Modules:
  0.0 585.8 jit_solution(4994581305114566087)
XLA Ops:
  7.2 2.2 stack.2
  9.4 12.0 %all-to-all-start = ((bf16[32,32,896]{2,1,0:T(8,128)(2,1)}), bf16[32,32,896]{2,1,0:T(8,128)(2,1)S(1)}, u32[]{:S(2)}, u32[]{:S(2)}) async-start(bf16[32,32,896]{2,1,0:T(8,128)(2,1)} %stack.2), calls=%async_computation | async-start | bytes 3670016 | tf_op jit(solution)/shard_map/all_to_all | solution.py:90
  21.4 0.0 reduce-scatter.5.cloned.1.call-start
  21.6 4.8 multiply_convert_fusion.1
  26.4 44.1 %all-to-all-done = bf16[32,32,896]{2,1,0:T(8,128)(2,1)S(1)} async-done(((bf16[32,32,896]{2,1,0:T(8,128)(2,1)}), bf16[32,32,896]{2,1,0:T(8,128)(2,1)S(1)}, u32[]{:S(2)}, u32[]{:S(2)}) %all-to-all-start) | async-done | bytes 1835040 | tf_op jit(solution)/shard_map/all_to_all | solution.py:90
  70.5 11.5 %convolution_bitcast_fusion = f32[1024,2304]{0,1:T(8,128)} fusion(bf16[1024,896]{1,0:T(8,128)(2,1)S(1)} %bitcast.22, bf16[896,576]{0,1:T(8,128)(2,1)} %get-tuple-element.18, bf16[896,576]{0,1:T(8,128)(2,1)} %get-tuple-element.19, bf16[896,576]{0,1:T(8,128)(2,1)} %param.16, bf16[896,576]{0,1:T(8,128)(2,1)} %param.15), kind=kOutput, calls=%fused_computation | convolution fusion | flops 4244373504 | bytes 15400960 | tf_op jit(solution)/shard_map/dot_general | solution.py:98
  82.0 0.0 reduce-scatter.5.cloned.1.call-update
  82.1 98.8 %reduce-scatter.5.cloned.1.call-done = f32[128,2304]{0,1:T(8,128)} async-done(((f32[1024,2304]{0,1:T(8,128)}), f32[128,2304]{0,1:T(8,128)}) %reduce-scatter.5.cloned.1.call-update) | async-done | bytes 1179664 | tf_op jit(solution)/shard_map/reduce_scatter | solution.py:99
  180.9 1.4 fusion.13
  182.3 0.2 copy.20
  182.5 1.7 broadcast_in_dim.8
  184.3 6.0 %all-to-all-start.1 = ((bf16[8,128,1152]{2,1,0:T(8,128)(2,1)}), bf16[8,128,1152]{2,1,0:T(8,128)(2,1)S(1)}, u32[]{:S(2)}, u32[]{:S(2)}) async-start(bf16[8,128,1152]{2,1,0:T(8,128)(2,1)} %broadcast_in_dim.8), calls=%async_computation.2 | async-start | bytes 4718592 | tf_op jit(solution)/shard_map/all_to_all | solution.py:22
  190.2 0.0 reduce-scatter.7.cloned.1.call-start
  190.3 1.1 neg.24
  191.5 0.2 copy-done.5
  191.7 2.1 multiply_convert_fusion
  193.9 47.2 %all-to-all-done.1 = bf16[8,128,1152]{2,1,0:T(8,128)(2,1)S(1)} async-done(((bf16[8,128,1152]{2,1,0:T(8,128)(2,1)}), bf16[8,128,1152]{2,1,0:T(8,128)(2,1)S(1)}, u32[]{:S(2)}, u32[]{:S(2)}) %all-to-all-start.1) | async-done | bytes 2359328 | tf_op jit(solution)/shard_map/all_to_all | solution.py:22
  241.0 7.0 %fusion.8 = f32[1024,896]{1,0:T(8,128)} fusion(bf16[1024,1152]{1,0:T(8,128)(2,1)S(1)} %bitcast.20, bf16[576,896]{1,0:T(8,128)(2,1)} %multiply_convert_fusion, bf16[576,896]{1,0:T(8,128)(2,1)} %neg.24), kind=kOutput, calls=%fused_computation.11 | convolution fusion | flops 2118057984 | bytes 8093696 | tf_op jit(solution)/shard_map/dot_general | solution.py:108
  248.1 0.0 reduce-scatter.7.cloned.1.call-update
  248.1 0.0 reduce-scatter.9.cloned.1.call-start
  248.2 47.4 %reduce-scatter.7.cloned.1.call-done = f32[256,896]{1,0:T(8,128)} async-done(((f32[1024,896]{1,0:T(8,128)}), f32[256,896]{1,0:T(8,128)}) %reduce-scatter.7.cloned.1.call-update) | async-done | bytes 917520 | tf_op jit(solution)/shard_map/reduce_scatter | solution.py:32
  295.6 0.0 reduce-scatter.9.cloned.1.call-update
  295.6 0.0 reduce-scatter.11.cloned.1.call-start
  295.6 26.8 %reduce-scatter.9.cloned.1.call-done = f32[64,896]{1,0:T(8,128)} async-done(((f32[256,896]{1,0:T(8,128)}), f32[64,896]{1,0:T(8,128)}) %reduce-scatter.9.cloned.1.call-update) | async-done | bytes 229392 | tf_op jit(solution)/shard_map/reduce_scatter | solution.py:32
  322.4 0.0 reduce-scatter.11.cloned.1.call-update
  322.4 0.2 all-gather.2.cloned.1.call-start
  322.6 0.8 dynamic_slice.3
  323.4 23.2 %reduce-scatter.11.cloned.1.call-done = f32[32,896]{1,0:T(8,128)} async-done(((f32[64,896]{1,0:T(8,128)}), f32[32,896]{1,0:T(8,128)}) %reduce-scatter.11.cloned.1.call-update) | async-done | bytes 114704 | tf_op jit(solution)/shard_map/reduce_scatter | solution.py:32
  346.6 2.2 fusion.15
  348.8 0.0 all-gather.2.cloned.1.call-update
  348.8 85.6 %all-gather.2.cloned.1.call-done = bf16[1024,896]{1,0:T(8,128)(2,1)} async-done(((bf16[32,896]{1,0:T(8,128)(2,1)}), bf16[1024,896]{1,0:T(8,128)(2,1)}) %all-gather.2.cloned.1.call-update) | async-done | bytes 1835024 | tf_op jit(solution)/shard_map/all_gather | solution.py:119
  434.3 2.9 convolution_bitcast_fusion.1
  437.3 0.2 copy.25
  437.4 57.4 %all_to_all.20 = f32[8,128,576]{1,2,0:T(8,128)S(1)} all-to-all(f32[8,128,576]{1,2,0:T(8,128)S(1)} %bitcast.19), channel_id=1, replica_groups=mesh['dp_0'=4,'dp_1'=4,'dp_2'=2,'mp_0'=4,'mp_1'=2] {'mp_0','mp_1'}, dimensions={0} | all-to-all | bytes 4718592 | tf_op jit(solution)/shard_map/all_to_all | solution.py:50
  494.9 0.8 reduce_sum.19
  495.7 0.5 copy-done.1
  496.2 1.1 multiply_convert_fusion.4
  497.4 0.2 copy.22
  497.6 1.7 broadcast_in_dim.9
  499.3 8.4 %all-to-all-start.3 = ((bf16[8,128,1152]{2,1,0:T(8,128)(2,1)}), bf16[8,128,1152]{2,1,0:T(8,128)(2,1)}, u32[]{:S(2)}, u32[]{:S(2)}) async-start(bf16[8,128,1152]{2,1,0:T(8,128)(2,1)} %broadcast_in_dim.9), calls=%async_computation.7 | async-start | bytes 4718592 | tf_op jit(solution)/shard_map/all_to_all | solution.py:22
  507.7 7.7 %psum.35 = f32[]{:T(128)} all-reduce(f32[]{:T(128)} %get-tuple-element.17), channel_id=1, replica_groups=mesh['dp_0'=4,'dp_1'=4,'dp_2'=2,'mp_0'=4,'mp_1'=2] {'dp_0'}, use_global_device_ids=true, to_apply=%region_5.6 | all-reduce | flops 1 | bytes 8 | tf_op jit(solution)/shard_map/psum | solution.py:38
  515.3 8.5 %psum.36 = f32[]{:T(128)} all-reduce(f32[]{:T(128)} %psum.35), channel_id=1, replica_groups=mesh['dp_0'=4,'dp_1'=4,'dp_2'=2,'mp_0'=4,'mp_1'=2] {'dp_1'}, use_global_device_ids=true, to_apply=%region_6.7 | all-reduce | flops 1 | bytes 8 | tf_op jit(solution)/shard_map/psum | solution.py:38
  523.8 14.9 %psum.37 = f32[]{:T(128)} all-reduce(f32[]{:T(128)} %psum.36), channel_id=1, replica_groups=mesh['dp_0'=4,'dp_1'=4,'dp_2'=2,'mp_0'=4,'mp_1'=2] {'dp_2'}, use_global_device_ids=true, to_apply=%region_7.8 | all-reduce | flops 1 | bytes 8 | tf_op jit(solution)/shard_map/psum | solution.py:38
  538.7 23.5 %psum.38 = f32[]{:T(128)} all-reduce(f32[]{:T(128)} %psum.37), channel_id=1, replica_groups=mesh['dp_0'=4,'dp_1'=4,'dp_2'=2,'mp_0'=4,'mp_1'=2] {'mp_0'}, use_global_device_ids=true, to_apply=%region_8.9 | all-reduce | flops 1 | bytes 8 | tf_op jit(solution)/shard_map/psum | solution.py:38
  562.2 4.9 psum.39
  567.8 4.0 convolution_convert_fusion.1
  571.8 4.9 fusion.7
  576.7 1.5 fusion.18
  (35 shorter events, 0.2 us)
Async XLA Ops:
  9.4 12.1 %copy-start.8 = (s32[2,576]{1,0:T(2,128)S(1)}, s32[2,576]{1,0:T(2,128)}, u32[]{:S(2)}) copy-start(s32[2,576]{1,0:T(2,128)} %param.23) | copy-start | bytes 13828
  9.4 12.1 %copy-start.9 = (f32[2,576]{1,0:T(2,128)S(1)}, f32[2,576]{1,0:T(2,128)}, u32[]{:S(2)}) copy-start(f32[2,576]{1,0:T(2,128)} %param.21) | copy-start | bytes 13828
  9.4 12.2 %copy-start.10 = (s32[2,576]{1,0:T(2,128)S(1)}, s32[2,576]{1,0:T(2,128)}, u32[]{:S(2)}) copy-start(s32[2,576]{1,0:T(2,128)} %param.22) | copy-start | bytes 13828
  9.4 12.2 %copy-start.7 = (bf16[896,576]{0,1:T(8,128)(2,1)S(1)}, bf16[896,576]{0,1:T(8,128)(2,1)}, u32[]{:S(2)}) copy-start(bf16[896,576]{0,1:T(8,128)(2,1)} %param.19) | copy-start | bytes 3096580
  9.4 61.1 %all-to-all-start = ((bf16[32,32,896]{2,1,0:T(8,128)(2,1)}), bf16[32,32,896]{2,1,0:T(8,128)(2,1)S(1)}, u32[]{:S(2)}, u32[]{:S(2)}) async-start(bf16[32,32,896]{2,1,0:T(8,128)(2,1)} %stack.2), calls=%async_computation | async-start | bytes 3670016 | tf_op jit(solution)/shard_map/all_to_all | solution.py:90
  21.4 159.5 %reduce-scatter.5.cloned.1.call-start = ((), (), s32[]{:S(2)}) async-start(), calls=%async_computation.8 | async-start | bytes 10616832 | tf_op jit(solution)/shard_map/reduce_scatter | solution.py:99
  70.5 11.5 %copy-start.4 = (bf16[32,32,896]{2,1,0:T(8,128)(2,1)}, bf16[32,32,896]{2,1,0:T(8,128)(2,1)S(1)}, u32[]{:S(2)}) copy-start(bf16[32,32,896]{2,1,0:T(8,128)(2,1)S(1)} %all-to-all-done) | copy-start | bytes 5505028
  184.3 6.0 %copy-start.11 = (s32[896]{0:T(1024)S(1)}, s32[896]{0:T(1024)}, u32[]{:S(2)}) copy-start(s32[896]{0:T(1024)} %param.26) | copy-start | bytes 10756
  184.3 6.1 %copy-start = (bf16[576,896]{1,0:T(8,128)(2,1)S(1)}, bf16[576,896]{1,0:T(8,128)(2,1)}, u32[]{:S(2)}) copy-start(bf16[576,896]{1,0:T(8,128)(2,1)} %param.17) | copy-start | bytes 3096580
  184.3 56.8 %all-to-all-start.1 = ((bf16[8,128,1152]{2,1,0:T(8,128)(2,1)}), bf16[8,128,1152]{2,1,0:T(8,128)(2,1)S(1)}, u32[]{:S(2)}, u32[]{:S(2)}) async-start(bf16[8,128,1152]{2,1,0:T(8,128)(2,1)} %broadcast_in_dim.8), calls=%async_computation.2 | async-start | bytes 4718592 | tf_op jit(solution)/shard_map/all_to_all | solution.py:22
  190.2 1.2 copy-start.12
  190.2 1.2 copy-start.13
  190.2 105.3 %reduce-scatter.7.cloned.1.call-start = ((), (), s32[]{:S(2)}) async-start(), calls=%async_computation.9 | async-start | bytes 4587520 | tf_op jit(solution)/shard_map/reduce_scatter | solution.py:32
  190.3 1.4 copy-start.5
  241.0 7.0 %copy-start.2 = (bf16[8,128,1152]{2,1,0:T(8,128)(2,1)}, bf16[8,128,1152]{2,1,0:T(8,128)(2,1)S(1)}, u32[]{:S(2)}) copy-start(bf16[8,128,1152]{2,1,0:T(8,128)(2,1)S(1)} %all-to-all-done.1) | copy-start | bytes 7077892
  248.1 186.3 %copy-start.6 = (bf16[576,896]{1,0:T(8,128)(2,1)S(1)}, bf16[576,896]{1,0:T(8,128)(2,1)}, u32[]{:S(2)}) copy-start(bf16[576,896]{1,0:T(8,128)(2,1)} %multiply_convert_fusion) | copy-start | bytes 3096580
  248.1 74.3 %reduce-scatter.9.cloned.1.call-start = ((), (), s32[]{:S(2)}) async-start(), calls=%async_computation.10 | async-start | bytes 1146880 | tf_op jit(solution)/shard_map/reduce_scatter | solution.py:32
  295.6 51.0 %reduce-scatter.11.cloned.1.call-start = ((), (), s32[]{:S(2)}) async-start(), calls=%async_computation.11 | async-start | bytes 344064 | tf_op jit(solution)/shard_map/reduce_scatter | solution.py:32
  322.4 111.9 %all-gather.2.cloned.1.call-start = ((), (), s32[]{:S(2)}) async-start(), calls=%async_computation.12 | async-start | bytes 1892352 | tf_op jit(solution)/shard_map/all_gather | solution.py:119
  494.9 1.4 copy-start.1
  499.3 68.5 %copy-start.3 = (bf16[8,128,1152]{2,1,0:T(8,128)(2,1)S(1)}, bf16[8,128,1152]{2,1,0:T(8,128)(2,1)}, u32[]{:S(2)}) copy-start(bf16[8,128,1152]{2,1,0:T(8,128)(2,1)} %copy-done.2) | copy-start | bytes 7077892
  499.3 72.5 %all-to-all-start.3 = ((bf16[8,128,1152]{2,1,0:T(8,128)(2,1)}), bf16[8,128,1152]{2,1,0:T(8,128)(2,1)}, u32[]{:S(2)}, u32[]{:S(2)}) async-start(bf16[8,128,1152]{2,1,0:T(8,128)(2,1)} %broadcast_in_dim.9), calls=%async_computation.7 | async-start | bytes 4718592 | tf_op jit(solution)/shard_map/all_to_all | solution.py:22
Sparse Core Ops, SparseCore 0:
  82.2 98.6 reduce-scatter.4
  248.2 47.2 reduce-scatter.6
  298.1 24.2 reduce-scatter.8
  324.7 21.7 reduce-scatter.10
  350.4 83.9 all-gather.1
